TPU v7x, 256 devices: a whole 4x4x8 slice. The times are simulated.
256 devices in a mesh: site: 4 (over z_lo), py: 8 (over z_hi, x), px: 4 (over y), pz: 2 (over core).
Axes of the slice: x: 4, y: 4, z: 8 (z_hi: 2, z_lo: 4; z = z_hi * 4 + z_lo), core: 2. Of those that a mesh axis runs over, the one named last changes fastest.
Arguments:
- initial_heat_state: float32 [128, 256, 64, 128], P(('site', 'py'), 'px', 'pz'), parts along dimension 0, may hold values from 0.2 to 1.8
- scaled_speed_north: float32 [128, 256, 64, 128], P(('site', 'py'), 'px', 'pz'), parts along dimension 0, may hold values from -0.3 to 0.3
- scaled_speed_east: float32 [128, 256, 64, 128], P(('site', 'py'), 'px', 'pz'), parts along dimension 0, may hold values from -0.3 to 0.3
- scaled_speed_upward: float32 [128, 256, 64, 128], P(('site', 'py'), 'px', 'pz'), parts along dimension 0, may hold values from -0.3 to 0.3
Outputs:
- temperature_end: float32 [128, 256, 64, 128], P(('site', 'py'), 'px', 'pz'), parts along dimension 0
There are 4 independent parts, one for each index of `site`. A program takes and returns all parts, laid end to end along the dimension named above; each array names one. Nothing has to cross between parts.
All inputs are finite; a program needn't handle non-finite values.
Results may differ from a plain program's by a relative error of at most 0.00002.
Values sent between devices are 32-bit elements; how exact they have to be, the bound alone decides.
A program may use at most 256 MiB of HBM per device.

v0:
```python
import jax
import jax.numpy as jnp
from jax import lax
from jax.sharding import PartitionSpec as P

STEPS = 4


def extended(array, sides, width):
    edges = {}
    for axis, dim in sides:
        size, length = (lax.axis_size(axis), array.shape[dim])
        up = [(i, (i + 1) % size) for i in range(size - 1)]
        last = lax.slice_in_dim(array, length - width, length, axis=dim)
        initial = lax.slice_in_dim(array, 0, width, axis=dim)
        edges[dim] = (
            lax.ppermute(last, axis, up),
            lax.ppermute(initial, axis, [(b, a) for a, b in up]),
        )
    done = []
    for _, dim in sides:
        low, high = edges[dim]
        around = [(width, width) if d in done else (0, 0) for d in range(array.ndim)]
        array = jnp.concatenate([jnp.pad(low, around), array, jnp.pad(high, around)], axis=dim)
        done.append(dim)
    return array


def strip_edges(values, dims):
    for dim in dims:
        values = lax.slice_in_dim(values, 1, values.shape[dim] - 1, axis=dim)
    return values


def neighbour(values, dim, start, dims):
    others = [other for other in dims if other != dim]
    values = strip_edges(values, others)
    return lax.slice_in_dim(values, start, start + values.shape[dim] - 2, axis=dim)


def march_once(padded_with_frame, scaled_speed_north, scaled_speed_east, scaled_speed_upward):
    middle = strip_edges(padded_with_frame, (0, 1, 2))
    lower = [neighbour(padded_with_frame, dim, 0, (0, 1, 2)) for dim in (0, 1, 2)]
    upper = [neighbour(padded_with_frame, dim, 2, (0, 1, 2)) for dim in (0, 1, 2)]
    slopes = [above - below for above, below in zip(upper, lower)]
    smooth_rate = 0.05
    spread = lower[0] + upper[0] + lower[1] + upper[1] + lower[2] + upper[2] - 6.0 * middle
    return (
        middle
        - scaled_speed_north * slopes[0]
        - scaled_speed_east * slopes[1]
        - scaled_speed_upward * slopes[2]
        + smooth_rate * spread
    )


def body(initial_heat_state, scaled_speed_north, scaled_speed_east, scaled_speed_upward):
    for step in range(STEPS):
        padded_with_frame = extended(initial_heat_state, (("py", 0), ("px", 1), ("pz", 2)), 1)
        initial_heat_state = march_once(
            padded_with_frame, scaled_speed_north, scaled_speed_east, scaled_speed_upward
        )
    return initial_heat_state


def solution(mesh):
    in_specs = (
        P(("site", "py"), "px", "pz", None),
        P(("site", "py"), "px", "pz", None),
        P(("site", "py"), "px", "pz", None),
        P(("site", "py"), "px", "pz", None),
    )
    out_specs = P(("site", "py"), "px", "pz", None)
    return jax.shard_map(body, mesh=mesh, in_specs=in_specs, out_specs=out_specs, check_vma=False)
```

profile of v0, /device:TPU:160, one launch (start us, length us, event | category | flops | bytes accessed | tf_op | source)
XLA Modules:
  0.0 237.6 jit_solution(7531675795112923545)
XLA Ops:
  0.0 4.6 %copy.10 = f32[4,64,32,128]{3,1,2,0:T(8,128)S(1)} copy(f32[4,64,32,128]{3,2,1,0:T(8,128)} %param.4) | data formatting | bytes 8388608 | tf_op args[0]
  4.8 3.7 %collective-permute-start.1 = (f32[1,64,32,128]{3,1,2,0:T(8,128)S(1)}, f32[1,64,32,128]{3,1,2,0:T(8,128)S(1)}, u32[]{:S(2)}, u32[]{:S(2)}) collective-permute-start(f32[1,64,32,128]{3,1,2,0:T(8,128)S(1)} %get-tuple-element.28), channel_id=1, source_target_pairs={{0,8},{8,16},{16,24},{24,32},{32,40},{40,48},{48,56},{1,9},{9,17},... | collective-permute-start | bytes 3145736 | tf_op jit(solution)/shard_map/ppermute | solution.py:17
  8.4 8.5 %collective-permute-start = (f32[1,64,32,128]{3,1,2,0:T(8,128)S(1)}, f32[1,64,32,128]{3,1,2,0:T(8,128)S(1)}, u32[]{:S(2)}, u32[]{:S(2)}) collective-permute-start(f32[1,64,32,128]{3,1,2,0:T(8,128)S(1)} %get-tuple-element.27), channel_id=1, source_target_pairs={{8,0},{16,8},{24,16},{32,24},{40,32},{48,40},{56,48},{9,1},{17,9},... | collective-permute-start | bytes 3145736 | tf_op jit(solution)/shard_map/ppermute | solution.py:18
  18.2 4.5 %collective-permute-start.3 = (f32[4,1,32,128]{3,1,2,0:T(1,128)S(1)}, f32[4,1,32,128]{3,1,2,0:T(1,128)S(1)}, u32[]{:S(2)}, u32[]{:S(2)}) collective-permute-start(f32[4,1,32,128]{3,1,2,0:T(1,128)S(1)} %bitcast.2), channel_id=1, source_target_pairs={{0,2},{2,4},{4,6},{1,3},{3,5},{5,7},{8,10},{10,12},{12,14},{9,11},... | collective-permute-start | bytes 196616 | tf_op jit(solution)/shard_map/ppermute | solution.py:17
  24.1 3.0 %collective-permute-start.5 = (f32[4,64,1,128]{3,1,2,0:T(8,128)S(1)}, f32[4,64,1,128]{3,1,2,0:T(8,128)S(1)}, u32[]{:S(2)}, u32[]{:S(2)}) collective-permute-start(f32[4,64,1,128]{3,1,2,0:T(8,128)S(1)} %get-tuple-element.23), channel_id=1, source_target_pairs={{0,1},{2,3},{4,5},{6,7},{8,9},{10,11},{12,13},{14,15},{16,17},{18,... | collective-permute-start | bytes 393224 | tf_op jit(solution)/shard_map/ppermute | solution.py:17
  27.3 33.0 %collective-permute-done.1 = f32[1,64,32,128]{3,1,2,0:T(8,128)S(1)} collective-permute-done((f32[1,64,32,128]{3,1,2,0:T(8,128)S(1)}, f32[1,64,32,128]{3,1,2,0:T(8,128)S(1)}, u32[]{:S(2)}, u32[]{:S(2)}) %collective-permute-start.1) | collective-permute-done | bytes 1048608 | tf_op jit(solution)/shard_map/ppermute | solution.py:17
  60.5 2.4 %constant_dynamic-update-slice_fusion.1 = f32[6,64,32,128]{3,1,2,0:T(8,128)S(1)} fusion(f32[6,64,32,128]{3,1,2,0:T(8,128)S(1)} %constant_dynamic-update-slice_fusion.2, f32[4,64,32,128]{3,2,1,0:T(8,128)S(1)} %copy-done.3), kind=kLoop, calls=%fused_computation.79 | loop fusion | bytes 8388608
  65.0 15.5 %multiply_add_fusion.3 = f32[4,64,32,128]{3,1,2,0:T(8,128)S(1)} fusion(f32[4,64,32,128]{3,1,2,0:T(8,128)S(1)} %copy.10, f32[4,64,1,128]{3,1,2,0:T(8,128)S(1)} %collective-permute-done.4, f32[6,1,32,128]{3,1,2,0:T(1,128)S(1)} %pad.50, f32[6,64,32,128]{3,1,2,0:T(8,128)S(1)} %constant_dynamic-update-slice_fusion, f32[6,1,32,128]{3,1,2,0:T(1,128)S(1)} %pad.51, ...), kind=kLoop, calls=%fused_computation.77 | loop fusion | flops 35651584 | bytes 29818880 | tf_op jit(solution)/shard_map/add | solution.py:49
  80.7 7.1 %collective-permute-start.6 = (f32[1,64,32,128]{3,1,2,0:T(8,128)S(1)}, f32[1,64,32,128]{3,1,2,0:T(8,128)S(1)}, u32[]{:S(2)}, u32[]{:S(2)}) collective-permute-start(f32[1,64,32,128]{3,1,2,0:T(8,128)S(1)} %get-tuple-element.22), channel_id=1, source_target_pairs={{8,0},{16,8},{24,16},{32,24},{40,32},{48,40},{56,48},{9,1},{17,9},... | collective-permute-start | bytes 3145736 | tf_op jit(solution)/shard_map/ppermute | solution.py:18
  87.8 1.9 collective-permute-start.7
  92.5 3.0 %collective-permute-start.11 = (f32[4,64,1,128]{3,1,2,0:T(8,128)S(1)}, f32[4,64,1,128]{3,1,2,0:T(8,128)S(1)}, u32[]{:S(2)}, u32[]{:S(2)}) collective-permute-start(f32[4,64,1,128]{3,1,2,0:T(8,128)S(1)} %get-tuple-element.17), channel_id=1, source_target_pairs={{0,1},{2,3},{4,5},{6,7},{8,9},{10,11},{12,13},{14,15},{16,17},{18,... | collective-permute-start | bytes 393224 | tf_op jit(solution)/shard_map/ppermute | solution.py:17
  96.0 4.1 %collective-permute-start.9 = (f32[4,1,32,128]{3,1,2,0:T(1,128)S(1)}, f32[4,1,32,128]{3,1,2,0:T(1,128)S(1)}, u32[]{:S(2)}, u32[]{:S(2)}) collective-permute-start(f32[4,1,32,128]{3,1,2,0:T(1,128)S(1)} %get-tuple-element.19), channel_id=1, source_target_pairs={{0,2},{2,4},{4,6},{1,3},{3,5},{5,7},{8,10},{10,12},{12,14},{9,11},... | collective-permute-start | bytes 196616 | tf_op jit(solution)/shard_map/ppermute | solution.py:17
  100.2 1.8 collective-permute-done.9
  102.1 7.9 %collective-permute-done.6 = f32[1,64,32,128]{3,1,2,0:T(8,128)S(1)} collective-permute-done((f32[1,64,32,128]{3,1,2,0:T(8,128)S(1)}, f32[1,64,32,128]{3,1,2,0:T(8,128)S(1)}, u32[]{:S(2)}, u32[]{:S(2)}) %collective-permute-start.6) | collective-permute-done | bytes 1048608 | tf_op jit(solution)/shard_map/ppermute | solution.py:18
  110.0 10.1 %collective-permute-done.7 = f32[1,64,32,128]{3,1,2,0:T(8,128)S(1)} collective-permute-done((f32[1,64,32,128]{3,1,2,0:T(8,128)S(1)}, f32[1,64,32,128]{3,1,2,0:T(8,128)S(1)}, u32[]{:S(2)}, u32[]{:S(2)}) %collective-permute-start.7) | collective-permute-done | bytes 1048608 | tf_op jit(solution)/shard_map/ppermute | solution.py:17
  120.1 15.5 %multiply_add_fusion.2 = f32[4,64,32,128]{3,1,2,0:T(8,128)S(1)} fusion(f32[4,64,32,128]{3,1,2,0:T(8,128)S(1)} %multiply_add_fusion.3, f32[4,64,1,128]{3,1,2,0:T(8,128)S(1)} %collective-permute-done.10, f32[6,1,32,128]{3,1,2,0:T(1,128)S(1)} %pad.54, f32[1,64,32,128]{3,1,2,0:T(8,128)S(1)} %collective-permute-done.6, ...), kind=kLoop, calls=%fused_computation.76 | loop fusion | flops 44040192 | bytes 23527424 | tf_op jit(solution)/shard_map/add | solution.py:49
  135.9 1.9 collective-permute-start.12
  137.8 4.1 %collective-permute-start.13 = (f32[1,64,32,128]{3,1,2,0:T(8,128)S(1)}, f32[1,64,32,128]{3,1,2,0:T(8,128)S(1)}, u32[]{:S(2)}, u32[]{:S(2)}) collective-permute-start(f32[1,64,32,128]{3,1,2,0:T(8,128)S(1)} %get-tuple-element.15), channel_id=1, source_target_pairs={{0,8},{8,16},{16,24},{24,32},{32,40},{40,48},{48,56},{1,9},{9,17},... | collective-permute-start | bytes 3145736 | tf_op jit(solution)/shard_map/ppermute | solution.py:17
  144.7 3.0 %collective-permute-start.17 = (f32[4,64,1,128]{3,1,2,0:T(8,128)S(1)}, f32[4,64,1,128]{3,1,2,0:T(8,128)S(1)}, u32[]{:S(2)}, u32[]{:S(2)}) collective-permute-start(f32[4,64,1,128]{3,1,2,0:T(8,128)S(1)} %get-tuple-element.11), channel_id=1, source_target_pairs={{0,1},{2,3},{4,5},{6,7},{8,9},{10,11},{12,13},{14,15},{16,17},{18,... | collective-permute-start | bytes 393224 | tf_op jit(solution)/shard_map/ppermute | solution.py:17
  148.2 4.1 %collective-permute-start.15 = (f32[4,1,32,128]{3,1,2,0:T(1,128)S(1)}, f32[4,1,32,128]{3,1,2,0:T(1,128)S(1)}, u32[]{:S(2)}, u32[]{:S(2)}) collective-permute-start(f32[4,1,32,128]{3,1,2,0:T(1,128)S(1)} %get-tuple-element.13), channel_id=1, source_target_pairs={{0,2},{2,4},{4,6},{1,3},{3,5},{5,7},{8,10},{10,12},{12,14},{9,11},... | collective-permute-start | bytes 196616 | tf_op jit(solution)/shard_map/ppermute | solution.py:17
  154.3 7.1 %collective-permute-done.12 = f32[1,64,32,128]{3,1,2,0:T(8,128)S(1)} collective-permute-done((f32[1,64,32,128]{3,1,2,0:T(8,128)S(1)}, f32[1,64,32,128]{3,1,2,0:T(8,128)S(1)}, u32[]{:S(2)}, u32[]{:S(2)}) %collective-permute-start.12) | collective-permute-done | bytes 1048608 | tf_op jit(solution)/shard_map/ppermute | solution.py:18
  161.3 7.9 %collective-permute-done.13 = f32[1,64,32,128]{3,1,2,0:T(8,128)S(1)} collective-permute-done((f32[1,64,32,128]{3,1,2,0:T(8,128)S(1)}, f32[1,64,32,128]{3,1,2,0:T(8,128)S(1)}, u32[]{:S(2)}, u32[]{:S(2)}) %collective-permute-start.13) | collective-permute-done | bytes 1048608 | tf_op jit(solution)/shard_map/ppermute | solution.py:17
  169.3 15.5 %multiply_add_fusion.1 = f32[4,64,32,128]{3,1,2,0:T(8,128)S(1)} fusion(f32[4,64,32,128]{3,1,2,0:T(8,128)S(1)} %multiply_add_fusion.2, f32[4,64,1,128]{3,1,2,0:T(8,128)S(1)} %collective-permute-done.16, f32[6,1,32,128]{3,1,2,0:T(1,128)S(1)} %pad.58, f32[1,64,32,128]{3,1,2,0:T(8,128)S(1)} %collective-permute-done.12, ...), kind=kLoop, calls=%fused_computation.75 | loop fusion | flops 44040192 | bytes 23527424 | tf_op jit(solution)/shard_map/add | solution.py:49
  185.1 1.9 collective-permute-start.18
  187.0 3.9 %collective-permute-start.19 = (f32[1,64,32,128]{3,1,2,0:T(8,128)S(1)}, f32[1,64,32,128]{3,1,2,0:T(8,128)S(1)}, u32[]{:S(2)}, u32[]{:S(2)}) collective-permute-start(f32[1,64,32,128]{3,1,2,0:T(8,128)S(1)} %get-tuple-element.9), channel_id=1, source_target_pairs={{0,8},{8,16},{16,24},{24,32},{32,40},{40,48},{48,56},{1,9},{9,17},... | collective-permute-start | bytes 3145736 | tf_op jit(solution)/shard_map/ppermute | solution.py:17
  193.6 3.0 %collective-permute-start.23 = (f32[4,64,1,128]{3,1,2,0:T(8,128)S(1)}, f32[4,64,1,128]{3,1,2,0:T(8,128)S(1)}, u32[]{:S(2)}, u32[]{:S(2)}) collective-permute-start(f32[4,64,1,128]{3,1,2,0:T(8,128)S(1)} %get-tuple-element.5), channel_id=1, source_target_pairs={{0,1},{2,3},{4,5},{6,7},{8,9},{10,11},{12,13},{14,15},{16,17},{18,... | collective-permute-start | bytes 393224 | tf_op jit(solution)/shard_map/ppermute | solution.py:17
  197.2 4.1 %collective-permute-start.21 = (f32[4,1,32,128]{3,1,2,0:T(1,128)S(1)}, f32[4,1,32,128]{3,1,2,0:T(1,128)S(1)}, u32[]{:S(2)}, u32[]{:S(2)}) collective-permute-start(f32[4,1,32,128]{3,1,2,0:T(1,128)S(1)} %get-tuple-element.7), channel_id=1, source_target_pairs={{0,2},{2,4},{4,6},{1,3},{3,5},{5,7},{8,10},{10,12},{12,14},{9,11},... | collective-permute-start | bytes 196616 | tf_op jit(solution)/shard_map/ppermute | solution.py:17
  201.3 1.8 collective-permute-done.21
  203.2 6.4 %collective-permute-done.18 = f32[1,64,32,128]{3,1,2,0:T(8,128)S(1)} collective-permute-done((f32[1,64,32,128]{3,1,2,0:T(8,128)S(1)}, f32[1,64,32,128]{3,1,2,0:T(8,128)S(1)}, u32[]{:S(2)}, u32[]{:S(2)}) %collective-permute-start.18) | collective-permute-done | bytes 1048608 | tf_op jit(solution)/shard_map/ppermute | solution.py:18
  209.6 7.9 %collective-permute-done.19 = f32[1,64,32,128]{3,1,2,0:T(8,128)S(1)} collective-permute-done((f32[1,64,32,128]{3,1,2,0:T(8,128)S(1)}, f32[1,64,32,128]{3,1,2,0:T(8,128)S(1)}, u32[]{:S(2)}, u32[]{:S(2)}) %collective-permute-start.19) | collective-permute-done | bytes 1048608 | tf_op jit(solution)/shard_map/ppermute | solution.py:17
  217.6 15.5 %multiply_add_fusion = f32[4,64,32,128]{3,1,2,0:T(8,128)S(1)} fusion(f32[4,64,32,128]{3,1,2,0:T(8,128)S(1)} %multiply_add_fusion.1, f32[4,64,1,128]{3,1,2,0:T(8,128)S(1)} %collective-permute-done.22, f32[6,1,32,128]{3,1,2,0:T(1,128)S(1)} %pad.62, f32[1,64,32,128]{3,1,2,0:T(8,128)S(1)} %collective-permute-done.18, ...), kind=kLoop, calls=%fused_computation.74 | loop fusion | flops 44040192 | bytes 23527424 | tf_op jit(solution)/shard_map/add | solution.py:49
  233.1 4.4 %copy.28 = f32[4,64,32,128]{3,2,1,0:T(8,128)} copy(f32[4,64,32,128]{3,1,2,0:T(8,128)S(1)} %multiply_add_fusion) | data formatting | bytes 8388608 | tf_op jit(solution)/shard_map/add | solution.py:49
  (53 shorter events, 17.5 us)
Async XLA Ops:
  4.6 12.3 %copy-start.3 = (f32[4,64,32,128]{3,2,1,0:T(8,128)S(1)}, f32[4,64,32,128]{3,2,1,0:T(8,128)}, u32[]{:S(2)}) copy-start(f32[4,64,32,128]{3,2,1,0:T(8,128)} %param.4) | copy-start | bytes 12582916
  4.8 55.5 %collective-permute-start.1 = (f32[1,64,32,128]{3,1,2,0:T(8,128)S(1)}, f32[1,64,32,128]{3,1,2,0:T(8,128)S(1)}, u32[]{:S(2)}, u32[]{:S(2)}) collective-permute-start(f32[1,64,32,128]{3,1,2,0:T(8,128)S(1)} %get-tuple-element.28), channel_id=1, source_target_pairs={{0,8},{8,16},{16,24},{24,32},{32,40},{40,48},{48,56},{1,9},{9,17},... | collective-permute-start | bytes 3145736 | tf_op jit(solution)/shard_map/ppermute | solution.py:17
  8.4 54.4 %collective-permute-start = (f32[1,64,32,128]{3,1,2,0:T(8,128)S(1)}, f32[1,64,32,128]{3,1,2,0:T(8,128)S(1)}, u32[]{:S(2)}, u32[]{:S(2)}) collective-permute-start(f32[1,64,32,128]{3,1,2,0:T(8,128)S(1)} %get-tuple-element.27), channel_id=1, source_target_pairs={{8,0},{16,8},{24,16},{32,24},{40,32},{48,40},{56,48},{9,1},{17,9},... | collective-permute-start | bytes 3145736 | tf_op jit(solution)/shard_map/ppermute | solution.py:18
  16.9 7.2 %collective-permute-start.2 = (f32[4,1,32,128]{3,1,2,0:T(1,128)S(1)}, f32[4,1,32,128]{3,1,2,0:T(1,128)S(1)}, u32[]{:S(2)}, u32[]{:S(2)}) collective-permute-start(f32[4,1,32,128]{3,1,2,0:T(1,128)S(1)} %bitcast.3), channel_id=1, source_target_pairs={{2,0},{4,2},{6,4},{3,1},{5,3},{7,5},{10,8},{12,10},{14,12},{11,9},... | collective-permute-start | bytes 196616 | tf_op jit(solution)/shard_map/ppermute | solution.py:18
  18.2 9.0 %collective-permute-start.3 = (f32[4,1,32,128]{3,1,2,0:T(1,128)S(1)}, f32[4,1,32,128]{3,1,2,0:T(1,128)S(1)}, u32[]{:S(2)}, u32[]{:S(2)}) collective-permute-start(f32[4,1,32,128]{3,1,2,0:T(1,128)S(1)} %bitcast.2), channel_id=1, source_target_pairs={{0,2},{2,4},{4,6},{1,3},{3,5},{5,7},{8,10},{10,12},{12,14},{9,11},... | collective-permute-start | bytes 196616 | tf_op jit(solution)/shard_map/ppermute | solution.py:17
  22.8 40.2 %collective-permute-start.4 = (f32[4,64,1,128]{3,1,2,0:T(8,128)S(1)}, f32[4,64,1,128]{3,1,2,0:T(8,128)S(1)}, u32[]{:S(2)}, u32[]{:S(2)}) collective-permute-start(f32[4,64,1,128]{3,1,2,0:T(8,128)S(1)} %get-tuple-element.24), channel_id=1, source_target_pairs={{1,0},{3,2},{5,4},{7,6},{9,8},{11,10},{13,12},{15,14},{17,16},{19,... | collective-permute-start | bytes 393224 | tf_op jit(solution)/shard_map/ppermute | solution.py:18
  24.1 38.9 %collective-permute-start.5 = (f32[4,64,1,128]{3,1,2,0:T(8,128)S(1)}, f32[4,64,1,128]{3,1,2,0:T(8,128)S(1)}, u32[]{:S(2)}, u32[]{:S(2)}) collective-permute-start(f32[4,64,1,128]{3,1,2,0:T(8,128)S(1)} %get-tuple-element.23), channel_id=1, source_target_pairs={{0,1},{2,3},{4,5},{6,7},{8,9},{10,11},{12,13},{14,15},{16,17},{18,... | collective-permute-start | bytes 393224 | tf_op jit(solution)/shard_map/ppermute | solution.py:17
  60.3 2.7 %copy-start.2 = (f32[4,64,32,128]{3,2,1,0:T(8,128)S(1)}, f32[4,64,32,128]{3,2,1,0:T(8,128)}, u32[]{:S(2)}) copy-start(f32[4,64,32,128]{3,2,1,0:T(8,128)} %param.5) | copy-start | bytes 12582916
  60.4 3.4 %copy-start = (f32[4,64,32,128]{3,2,1,0:T(8,128)S(1)}, f32[4,64,32,128]{3,2,1,0:T(8,128)}, u32[]{:S(2)}) copy-start(f32[4,64,32,128]{3,2,1,0:T(8,128)} %param.7) | copy-start | bytes 12582916
  60.4 4.6 %copy-start.1 = (f32[4,64,32,128]{3,2,1,0:T(8,128)S(1)}, f32[4,64,32,128]{3,2,1,0:T(8,128)}, u32[]{:S(2)}) copy-start(f32[4,64,32,128]{3,2,1,0:T(8,128)} %param.6) | copy-start | bytes 12582916
  80.7 29.3 %collective-permute-start.6 = (f32[1,64,32,128]{3,1,2,0:T(8,128)S(1)}, f32[1,64,32,128]{3,1,2,0:T(8,128)S(1)}, u32[]{:S(2)}, u32[]{:S(2)}) collective-permute-start(f32[1,64,32,128]{3,1,2,0:T(8,128)S(1)} %get-tuple-element.22), channel_id=1, source_target_pairs={{8,0},{16,8},{24,16},{32,24},{40,32},{48,40},{56,48},{9,1},{17,9},... | collective-permute-start | bytes 3145736 | tf_op jit(solution)/shard_map/ppermute | solution.py:18
  87.8 32.3 %collective-permute-start.7 = (f32[1,64,32,128]{3,1,2,0:T(8,128)S(1)}, f32[1,64,32,128]{3,1,2,0:T(8,128)S(1)}, u32[]{:S(2)}, u32[]{:S(2)}) collective-permute-start(f32[1,64,32,128]{3,1,2,0:T(8,128)S(1)} %get-tuple-element.21), channel_id=1, source_target_pairs={{0,8},{8,16},{16,24},{24,32},{32,40},{40,48},{48,56},{1,9},{9,17},... | collective-permute-start | bytes 3145736 | tf_op jit(solution)/shard_map/ppermute | solution.py:17
  89.9 6.2 %collective-permute-start.8 = (f32[4,1,32,128]{3,1,2,0:T(1,128)S(1)}, f32[4,1,32,128]{3,1,2,0:T(1,128)S(1)}, u32[]{:S(2)}, u32[]{:S(2)}) collective-permute-start(f32[4,1,32,128]{3,1,2,0:T(1,128)S(1)} %get-tuple-element.20), channel_id=1, source_target_pairs={{2,0},{4,2},{6,4},{3,1},{5,3},{7,5},{10,8},{12,10},{14,12},{11,9},... | collective-permute-start | bytes 196616 | tf_op jit(solution)/shard_map/ppermute | solution.py:18
  91.2 10.9 %collective-permute-start.10 = (f32[4,64,1,128]{3,1,2,0:T(8,128)S(1)}, f32[4,64,1,128]{3,1,2,0:T(8,128)S(1)}, u32[]{:S(2)}, u32[]{:S(2)}) collective-permute-start(f32[4,64,1,128]{3,1,2,0:T(8,128)S(1)} %get-tuple-element.18), channel_id=1, source_target_pairs={{1,0},{3,2},{5,4},{7,6},{9,8},{11,10},{13,12},{15,14},{17,16},{19,... | collective-permute-start | bytes 393224 | tf_op jit(solution)/shard_map/ppermute | solution.py:18
  92.5 9.6 %collective-permute-start.11 = (f32[4,64,1,128]{3,1,2,0:T(8,128)S(1)}, f32[4,64,1,128]{3,1,2,0:T(8,128)S(1)}, u32[]{:S(2)}, u32[]{:S(2)}) collective-permute-start(f32[4,64,1,128]{3,1,2,0:T(8,128)S(1)} %get-tuple-element.17), channel_id=1, source_target_pairs={{0,1},{2,3},{4,5},{6,7},{8,9},{10,11},{12,13},{14,15},{16,17},{18,... | collective-permute-start | bytes 393224 | tf_op jit(solution)/shard_map/ppermute | solution.py:17
  96.0 6.0 %collective-permute-start.9 = (f32[4,1,32,128]{3,1,2,0:T(1,128)S(1)}, f32[4,1,32,128]{3,1,2,0:T(1,128)S(1)}, u32[]{:S(2)}, u32[]{:S(2)}) collective-permute-start(f32[4,1,32,128]{3,1,2,0:T(1,128)S(1)} %get-tuple-element.19), channel_id=1, source_target_pairs={{0,2},{2,4},{4,6},{1,3},{3,5},{5,7},{8,10},{10,12},{12,14},{9,11},... | collective-permute-start | bytes 196616 | tf_op jit(solution)/shard_map/ppermute | solution.py:17
  135.9 25.4 %collective-permute-start.12 = (f32[1,64,32,128]{3,1,2,0:T(8,128)S(1)}, f32[1,64,32,128]{3,1,2,0:T(8,128)S(1)}, u32[]{:S(2)}, u32[]{:S(2)}) collective-permute-start(f32[1,64,32,128]{3,1,2,0:T(8,128)S(1)} %get-tuple-element.16), channel_id=1, source_target_pairs={{8,0},{16,8},{24,16},{32,24},{40,32},{48,40},{56,48},{9,1},{17,9},... | collective-permute-start | bytes 3145736 | tf_op jit(solution)/shard_map/ppermute | solution.py:18
  137.8 31.4 %collective-permute-start.13 = (f32[1,64,32,128]{3,1,2,0:T(8,128)S(1)}, f32[1,64,32,128]{3,1,2,0:T(8,128)S(1)}, u32[]{:S(2)}, u32[]{:S(2)}) collective-permute-start(f32[1,64,32,128]{3,1,2,0:T(8,128)S(1)} %get-tuple-element.15), channel_id=1, source_target_pairs={{0,8},{8,16},{16,24},{24,32},{32,40},{40,48},{48,56},{1,9},{9,17},... | collective-permute-start | bytes 3145736 | tf_op jit(solution)/shard_map/ppermute | solution.py:17
  142.0 6.2 %collective-permute-start.14 = (f32[4,1,32,128]{3,1,2,0:T(1,128)S(1)}, f32[4,1,32,128]{3,1,2,0:T(1,128)S(1)}, u32[]{:S(2)}, u32[]{:S(2)}) collective-permute-start(f32[4,1,32,128]{3,1,2,0:T(1,128)S(1)} %get-tuple-element.14), channel_id=1, source_target_pairs={{2,0},{4,2},{6,4},{3,1},{5,3},{7,5},{10,8},{12,10},{14,12},{11,9},... | collective-permute-start | bytes 196616 | tf_op jit(solution)/shard_map/ppermute | solution.py:18
  143.4 10.9 %collective-permute-start.16 = (f32[4,64,1,128]{3,1,2,0:T(8,128)S(1)}, f32[4,64,1,128]{3,1,2,0:T(8,128)S(1)}, u32[]{:S(2)}, u32[]{:S(2)}) collective-permute-start(f32[4,64,1,128]{3,1,2,0:T(8,128)S(1)} %get-tuple-element.12), channel_id=1, source_target_pairs={{1,0},{3,2},{5,4},{7,6},{9,8},{11,10},{13,12},{15,14},{17,16},{19,... | collective-permute-start | bytes 393224 | tf_op jit(solution)/shard_map/ppermute | solution.py:18
  144.7 9.6 %collective-permute-start.17 = (f32[4,64,1,128]{3,1,2,0:T(8,128)S(1)}, f32[4,64,1,128]{3,1,2,0:T(8,128)S(1)}, u32[]{:S(2)}, u32[]{:S(2)}) collective-permute-start(f32[4,64,1,128]{3,1,2,0:T(8,128)S(1)} %get-tuple-element.11), channel_id=1, source_target_pairs={{0,1},{2,3},{4,5},{6,7},{8,9},{10,11},{12,13},{14,15},{16,17},{18,... | collective-permute-start | bytes 393224 | tf_op jit(solution)/shard_map/ppermute | solution.py:17
  148.2 6.0 %collective-permute-start.15 = (f32[4,1,32,128]{3,1,2,0:T(1,128)S(1)}, f32[4,1,32,128]{3,1,2,0:T(1,128)S(1)}, u32[]{:S(2)}, u32[]{:S(2)}) collective-permute-start(f32[4,1,32,128]{3,1,2,0:T(1,128)S(1)} %get-tuple-element.13), channel_id=1, source_target_pairs={{0,2},{2,4},{4,6},{1,3},{3,5},{5,7},{8,10},{10,12},{12,14},{9,11},... | collective-permute-start | bytes 196616 | tf_op jit(solution)/shard_map/ppermute | solution.py:17
  185.1 24.6 %collective-permute-start.18 = (f32[1,64,32,128]{3,1,2,0:T(8,128)S(1)}, f32[1,64,32,128]{3,1,2,0:T(8,128)S(1)}, u32[]{:S(2)}, u32[]{:S(2)}) collective-permute-start(f32[1,64,32,128]{3,1,2,0:T(8,128)S(1)} %get-tuple-element.10), channel_id=1, source_target_pairs={{8,0},{16,8},{24,16},{32,24},{40,32},{48,40},{56,48},{9,1},{17,9},... | collective-permute-start | bytes 3145736 | tf_op jit(solution)/shard_map/ppermute | solution.py:18
  187.0 30.6 %collective-permute-start.19 = (f32[1,64,32,128]{3,1,2,0:T(8,128)S(1)}, f32[1,64,32,128]{3,1,2,0:T(8,128)S(1)}, u32[]{:S(2)}, u32[]{:S(2)}) collective-permute-start(f32[1,64,32,128]{3,1,2,0:T(8,128)S(1)} %get-tuple-element.9), channel_id=1, source_target_pairs={{0,8},{8,16},{16,24},{24,32},{32,40},{40,48},{48,56},{1,9},{9,17},... | collective-permute-start | bytes 3145736 | tf_op jit(solution)/shard_map/ppermute | solution.py:17
  191.0 6.2 %collective-permute-start.20 = (f32[4,1,32,128]{3,1,2,0:T(1,128)S(1)}, f32[4,1,32,128]{3,1,2,0:T(1,128)S(1)}, u32[]{:S(2)}, u32[]{:S(2)}) collective-permute-start(f32[4,1,32,128]{3,1,2,0:T(1,128)S(1)} %get-tuple-element.8), channel_id=1, source_target_pairs={{2,0},{4,2},{6,4},{3,1},{5,3},{7,5},{10,8},{12,10},{14,12},{11,9},... | collective-permute-start | bytes 196616 | tf_op jit(solution)/shard_map/ppermute | solution.py:18
  192.3 10.9 %collective-permute-start.22 = (f32[4,64,1,128]{3,1,2,0:T(8,128)S(1)}, f32[4,64,1,128]{3,1,2,0:T(8,128)S(1)}, u32[]{:S(2)}, u32[]{:S(2)}) collective-permute-start(f32[4,64,1,128]{3,1,2,0:T(8,128)S(1)} %get-tuple-element.6), channel_id=1, source_target_pairs={{1,0},{3,2},{5,4},{7,6},{9,8},{11,10},{13,12},{15,14},{17,16},{19,... | collective-permute-start | bytes 393224 | tf_op jit(solution)/shard_map/ppermute | solution.py:18
  193.6 9.6 %collective-permute-start.23 = (f32[4,64,1,128]{3,1,2,0:T(8,128)S(1)}, f32[4,64,1,128]{3,1,2,0:T(8,128)S(1)}, u32[]{:S(2)}, u32[]{:S(2)}) collective-permute-start(f32[4,64,1,128]{3,1,2,0:T(8,128)S(1)} %get-tuple-element.5), channel_id=1, source_target_pairs={{0,1},{2,3},{4,5},{6,7},{8,9},{10,11},{12,13},{14,15},{16,17},{18,... | collective-permute-start | bytes 393224 | tf_op jit(solution)/shard_map/ppermute | solution.py:17
  197.2 6.0 %collective-permute-start.21 = (f32[4,1,32,128]{3,1,2,0:T(1,128)S(1)}, f32[4,1,32,128]{3,1,2,0:T(1,128)S(1)}, u32[]{:S(2)}, u32[]{:S(2)}) collective-permute-start(f32[4,1,32,128]{3,1,2,0:T(1,128)S(1)} %get-tuple-element.7), channel_id=1, source_target_pairs={{0,2},{2,4},{4,6},{1,3},{3,5},{5,7},{8,10},{10,12},{12,14},{9,11},... | collective-permute-start | bytes 196616 | tf_op jit(solution)/shard_map/ppermute | solution.py:17
where the time goes:
time: 238 us
  waiting for transfers between devices  87.4 us (37%)
  starting transfers between devices  72.3 us (30%)
  other arithmetic  62 us (26%)
  local copies, waits for them, and re-layouts  15.4 us (6%)
    ppermute x12, waiting for transfers between devices, extended(): lax.ppermute(last, axis, up)  64.5 us
    add x4, other arithmetic, march_once(): middle - scaled_speed_north * slopes[0] - scaled_speed_east * slopes[1]  62 us
    ppermute x12, starting transfers between devices, extended(): lax.ppermute(last, axis, up)  42.6 us
    ppermute x12, starting transfers between devices, extended(): lax.ppermute(initial, axis, [(b, a) for a, b in up])  29.7 us
    ppermute x12, waiting for transfers between devices, extended(): lax.ppermute(initial, axis, [(b, a) for a, b in up])  22.9 us
    unnamed x11, local copies, waits for them, and re-layouts  9.13 us
  transfers between devices with their start and end apart: 24, of which 13 were waited for; matrix products, arithmetic and copies ran while one was open for 1% of the time, Pallas kernels for 0%

commit v1 on v0

v1 whole, which is shorter than its diff:
```python
import functools

import jax
import jax.numpy as jnp
from jax import lax
from jax.experimental import pallas as pl
from jax.experimental.pallas import tpu as pltpu
from jax.sharding import PartitionSpec as P

MESH = pl.DeviceIdType.MESH
STEPS = 4
NY, NX, NZ, NS = 4, 64, 32, 128
K = 16
XC = NX // K
DIRECT = 2
ZP = 8


def kernel(u, vn, ve, vu, out, U, V, H, *sems):
    (u_sem, v_sem, out_sem, h_send, h_recv, x_send, x_recv, z_send, z_recv) = sems
    py, px, pz = lax.axis_index("py"), lax.axis_index("px"), lax.axis_index("pz")
    has_lo, has_hi = py > 0, py < 7
    x_lo, x_hi = px > 0, px < 3
    relayed = pz == 1
    edge = (py == 0) | (py == 7)
    middle = (py == 3) | (py == 4)

    def chunk(i):
        half = i // 2
        return half + (i % 2) * (K - 1 - 2 * half)

    def cols(k):
        return pl.ds(k * XC, XC)

    def inner(k):
        return pl.ds(1 + k * XC, XC)

    def load_u(k):
        return pltpu.make_async_copy(
            u.at[:, cols(k)], U.at[0, :, inner(k), pl.ds(ZP, NZ)], u_sem.at[k]
        )

    def load_v(f, k):
        return pltpu.make_async_copy(
            (vn, ve, vu)[f].at[:, cols(k)], V.at[f, :, cols(k)], v_sem.at[f, k]
        )

    def store(k):
        return pltpu.make_async_copy(
            U.at[STEPS, :, inner(k), pl.ds(ZP, NZ)], out.at[:, cols(k)], out_sem.at[k]
        )

    def y_source(first, t, side, k):
        plane = (0, NY - 1)[side]
        if first:
            return u.at[plane, cols(k)]
        return U.at[t, plane, inner(k), pl.ds(ZP, NZ)]

    def y_copy(first, t, side, k, target, slot):
        return pltpu.make_async_remote_copy(
            src_ref=y_source(first, t, side, k),
            dst_ref=H.at[t, slot, cols(k)],
            send_sem=h_send.at[t, side, k],
            recv_sem=h_recv.at[t, slot, k],
            device_id={"py": target},
            device_id_type=MESH,
        )

    def through(t, i):
        late = (t == STEPS - 1) & (i >= K - DIRECT)
        return relayed & jnp.logical_not(late)

    def y_route(t, i, side):
        if side == 0:
            return jnp.where((py == 4) & through(t, i), 7, jnp.maximum(py - 1, 0)), 1
        return jnp.where((py == 3) & through(t, i), 0, jnp.minimum(py + 1, 7)), 0

    def send_y(first, t, i, k):
        @pl.when(has_lo)
        def _():
            y_copy(first, t, 0, k, *y_route(t, i, 0)).start()

        @pl.when(has_hi)
        def _():
            y_copy(first, t, 1, k, *y_route(t, i, 1)).start()

    def relay_copy(t, k):
        slot = jnp.where(py == 0, 0, 1)
        return pltpu.make_async_remote_copy(
            src_ref=H.at[t, slot, cols(k)],
            dst_ref=H.at[t, slot, cols(k)],
            send_sem=h_send.at[t, slot, k],
            recv_sem=h_recv.at[t, slot, k],
            device_id={"py": jnp.where(py == 0, 4, 3)},
            device_id_type=MESH,
        )

    def y_landed(t, slot, k):
        return pltpu.make_async_remote_copy(
            src_ref=H.at[t, slot, cols(k)],
            dst_ref=H.at[t, slot, cols(k)],
            send_sem=h_send.at[t, slot, k],
            recv_sem=h_recv.at[t, slot, k],
            device_id={"py": jnp.where(py == 0, 1, 0)},
            device_id_type=MESH,
        )

    def x_copy(first, t, side):
        src, dst = ((0, NX + 1), (NX - 1, 0))[side]
        source = u.at[:, src] if first else U.at[t, :, 1 + src, pl.ds(ZP, NZ)]
        return pltpu.make_async_remote_copy(
            src_ref=source,
            dst_ref=U.at[t, :, dst, pl.ds(ZP, NZ)],
            send_sem=x_send.at[t, side],
            recv_sem=x_recv.at[t, 1 - side],
            device_id={"px": (jnp.maximum(px - 1, 0), jnp.minimum(px + 1, 3))[side]},
            device_id_type=MESH,
        )

    def z_copy(first, t, k):
        start = pl.multiple_of((1 - pz) * (NZ - ZP), ZP)
        if first:
            source = u.at[:, cols(k), pl.ds(start, ZP)]
        else:
            source = U.at[t, :, inner(k), pl.ds(pl.multiple_of(start + ZP, ZP), ZP)]
        land = pl.multiple_of(pz * (NZ + ZP), ZP)
        return pltpu.make_async_remote_copy(
            src_ref=source,
            dst_ref=U.at[t, :, inner(k), pl.ds(land, ZP)],
            send_sem=z_send.at[t, k],
            recv_sem=z_recv.at[t, k],
            device_id={"pz": 1 - pz},
            device_id_type=MESH,
        )

    for i in range(K):
        load_u(chunk(i)).start()
    for i in range(K):
        for f in range(3):
            load_v(f, chunk(i)).start()

    barrier = pltpu.get_barrier_semaphore()

    def greet(cond, **where):
        @pl.when(cond)
        def _():
            pl.semaphore_signal(barrier, inc=1, device_id=where, device_id_type=MESH)

    greet(has_lo, py=jnp.maximum(py - 1, 0))
    greet(has_hi, py=jnp.minimum(py + 1, 7))
    greet(x_lo, px=jnp.maximum(px - 1, 0))
    greet(x_hi, px=jnp.minimum(px + 1, 3))
    greet(pz >= 0, pz=1 - pz)
    extra = relayed & (edge | middle)
    greet(extra, py=jnp.where(edge, 3, 0))
    greet(extra, py=jnp.where(edge, 4, 7))
    one = lambda c: c.astype(jnp.int32)
    peers = one(has_lo) + one(has_hi) + one(x_lo) + one(x_hi) + 1 + 2 * one(extra)
    pl.semaphore_wait(barrier, peers)

    @pl.when(x_lo)
    def _():
        x_copy(True, 0, 0).start()

    @pl.when(x_hi)
    def _():
        x_copy(True, 0, 1).start()

    def first_sends(i, _):
        k = chunk(i)
        send_y(True, 0, i, k)
        z_copy(True, 0, k).start()
        return 0

    lax.fori_loop(0, K, first_sends, 0)

    zero_slab = pl.multiple_of(pz * (NZ + ZP), ZP)

    def clear_z(n, _):
        t, y = n // NY, n % NY
        U[t, y, :, pl.ds(zero_slab, ZP), :] = jnp.zeros((NX + 2, ZP, NS), jnp.float32)
        return 0

    lax.fori_loop(0, STEPS * NY, clear_z, 0)

    def clear_x(cond, column):
        @pl.when(cond)
        def _():
            for t in range(STEPS):
                U[t, :, column, pl.ds(ZP, NZ), :] = jnp.zeros((NY, NZ, NS), jnp.float32)

    clear_x(jnp.logical_not(x_lo), 0)
    clear_x(jnp.logical_not(x_hi), NX + 1)

    def compute(t, k):
        def column(n, _):
            x = k * XC + n
            mid = pl.ds(ZP, NZ)
            lo = jnp.where(has_lo, H[t, 0, x], 0.0)
            hi = jnp.where(has_hi, H[t, 1, x], 0.0)
            c = [U[t, y, x + 1, mid, :] for y in range(NY)]
            around = [lo] + c + [hi]
            for y in range(NY):
                below, above = around[y], around[y + 2]
                left, right = U[t, y, x, mid, :], U[t, y, x + 2, mid, :]
                down = U[t, y, x + 1, pl.ds(ZP - 1, NZ), :]
                up = U[t, y, x + 1, pl.ds(ZP + 1, NZ), :]
                total = ((below + above) + (left + right)) + (down + up)
                flow = (
                    V[0, y, x] * (above - below)
                    + V[1, y, x] * (right - left)
                    + V[2, y, x] * (up - down)
                )
                spread = total - 6.0 * c[y]
                U[t + 1, y, x + 1, mid, :] = (c[y] - flow) + 0.05 * spread
            return 0

        lax.fori_loop(0, XC, column, 0)

    def sends(j):
        t, i = j // K, j % K
        k = chunk(i)

        @pl.when(t + 1 < STEPS)
        def _():
            send_y(False, t + 1, i, k)
            z_copy(False, t + 1, k).start()

            @pl.when((i == 0) & x_lo)
            def _():
                x_copy(False, t + 1, 0).start()

            @pl.when((i == 1) & x_hi)
            def _():
                x_copy(False, t + 1, 1).start()

        @pl.when(t + 1 == STEPS)
        def _():
            store(k).start()

    def iteration(j, _):
        t, i = j // K, j % K
        k = chunk(i)

        @pl.when(edge & through(t, i))
        def _():
            slot = jnp.where(py == 0, 0, 1)
            y_landed(t, slot, k).wait_recv()
            relay_copy(t, k).start()

        @pl.when(t == 0)
        def _():
            @pl.when(i == 0)
            def _():
                load_u(chunk(0)).wait()
                load_u(chunk(1)).wait()

            @pl.when(i + 2 < K)
            def _():
                load_u(chunk(jnp.minimum(i + 2, K - 1))).wait()

            for f in range(3):
                load_v(f, k).wait()

        @pl.when((i == 0) & x_lo)
        def _():
            x_landed(t, 0).wait_recv()

        @pl.when((i == 1) & x_hi)
        def _():
            x_landed(t, 1).wait_recv()

        z_copy(False, t, k).wait_recv()

        @pl.when(has_lo)
        def _():
            y_landed(t, 0, k).wait_recv()

        @pl.when(has_hi)
        def _():
            y_landed(t, 1, k).wait_recv()

        compute(t, k)

        @pl.when(j > 0)
        def _():
            sends(jnp.maximum(j - 1, 0))

        return 0

    def x_landed(t, side):
        column = (0, NX + 1)[side]
        return pltpu.make_async_remote_copy(
            src_ref=U.at[t, :, column, pl.ds(ZP, NZ)],
            dst_ref=U.at[t, :, column, pl.ds(ZP, NZ)],
            send_sem=x_send.at[t, side],
            recv_sem=x_recv.at[t, side],
            device_id={"px": jnp.where(px == 0, 1, 0)},
            device_id_type=MESH,
        )

    lax.fori_loop(0, STEPS * K, iteration, 0)
    sends(STEPS * K - 1)

    def finish(j, _):
        t, i = j // K, j % K
        k = chunk(i)

        @pl.when(has_lo | (edge & through(t, i)))
        def _():
            y_landed(t, 0, k).wait_send()

        @pl.when(has_hi | (edge & through(t, i)))
        def _():
            y_landed(t, 1, k).wait_send()

        z_copy(False, t, k).wait_send()
        return 0

    lax.fori_loop(0, STEPS * K, finish, 0)
    for t in range(STEPS):
        for side, there in ((0, x_lo), (1, x_hi)):

            @pl.when(there)
            def _():
                x_landed(t, side).wait_send()

    def stored(k, _):
        store(k).wait()
        return 0

    lax.fori_loop(0, K, stored, 0)


def body(u, vn, ve, vu):
    DMA = pltpu.SemaphoreType.DMA
    return pl.pallas_call(
        kernel,
        out_shape=jax.ShapeDtypeStruct(u.shape, u.dtype),
        in_specs=[pl.BlockSpec(memory_space=pl.ANY)] * 4,
        out_specs=pl.BlockSpec(memory_space=pl.ANY),
        scratch_shapes=[
            pltpu.VMEM((STEPS + 1, NY, NX + 2, NZ + 2 * ZP, NS), jnp.float32),
            pltpu.VMEM((3, NY, NX, NZ, NS), jnp.float32),
            pltpu.VMEM((STEPS, 2, NX, NZ, NS), jnp.float32),
            DMA((K,)),
            DMA((3, K)),
            DMA((K,)),
            DMA((STEPS, 2, K)),
            DMA((STEPS, 2, K)),
            DMA((STEPS, 2)),
            DMA((STEPS, 2)),
            DMA((STEPS, K)),
            DMA((STEPS, K)),
        ],
        compiler_params=pltpu.CompilerParams(
            collective_id=0, has_side_effects=True, vmem_limit_bytes=62 * 2**20
        ),
        name="march",
    )(u, vn, ve, vu)


def solution(mesh):
    spec = P(("site", "py"), "px", "pz", None)
    return jax.shard_map(
        body, mesh=mesh, in_specs=(spec,) * 4, out_specs=spec, check_vma=False
    )
```

time: 238 us -> 114 us (0.48)
  Pallas kernels: 0 us -> 109 us
  waiting for transfers between devices: 87.4 us -> 0 us
  starting transfers between devices: 72.3 us -> 0 us
  other arithmetic: 62 us -> 0 us
  local copies, waits for them, and re-layouts: 15.4 us -> 4.64 us
    pallas_call x0 -> x1, Pallas kernels: none -> 109 us  [body(): pl.pallas_call(kernel, out_shape=jax.ShapeDtypeStruct(u.shape, u.dtype),...]
    ppermute x24 -> x0, waiting for transfers between devices: 87.4 us -> none  [the longest x12 64.5 us: extended(): lax.ppermute(last, axis, up)]
    ppermute x24 -> x0, starting transfers between devices: 72.3 us -> none  [the longest x12 42.6 us: extended(): lax.ppermute(last, axis, up)]
    add x4 -> x0, other arithmetic: 62 us -> none  [march_once(): middle - scaled_speed_north * slopes[0] - scaled_speed_east * slopes[1]]
    unnamed x11 -> x1, local copies, waits for them, and re-layouts: 9.13 us -> 4.64 us
    add x1 -> x0, local copies, waits for them, and re-layouts: 4.44 us -> none  [march_once(): middle - scaled_speed_north * slopes[0] - scaled_speed_east * slopes[1]]
  transfers between devices with their start and end apart: 24 -> 0, of which waited for: 13 -> 0; matrix products, arithmetic and copies ran while one was open for 1% -> 0% of each run, Pallas kernels for 0% -> 0%
where the time goes in v1:
time: 114 us
  Pallas kernels  109 us (96%)
  local copies, waits for them, and re-layouts  4.64 us (4%)
    pallas_call x1, Pallas kernels, body(): pl.pallas_call(kernel, out_shape=jax.ShapeDtypeStruct(u.shape, u.dtype),...  109 us
    unnamed x1, local copies, waits for them, and re-layouts  4.64 us

profile of v1, /device:TPU:160, one launch (start us, length us, event | category | flops | bytes accessed | tf_op | source)
XLA Modules:
  0.0 113.6 jit_solution(9271024592347311534)
XLA Ops:
  0.0 109.0 %march.1 = f32[4,64,32,128]{3,2,1,0:T(8,128)} custom-call(f32[4,64,32,128]{3,2,1,0:T(8,128)} %u.1, f32[4,64,32,128]{3,2,1,0:T(8,128)} %vn.1, f32[4,64,32,128]{3,2,1,0:T(8,128)} %ve.1, f32[4,64,32,128]{3,2,1,0:T(8,128)} %vu.1), custom_call_target="tpu_custom_call" | custom-call | tf_op jit(solution)/shard_map/march/pallas_call | solution.py:337
  109.0 4.6 %copy.6 = f32[4,64,32,128]{3,2,1,0:T(8,128)} copy(f32[4,64,32,128]{3,2,1,0:T(8,128)} %march.1) | data formatting | bytes 8388608

commit v2 on v1

--- a/solution.py
+++ b/solution.py
@@ -10,9 +10,11 @@
 MESH = pl.DeviceIdType.MESH
 STEPS = 4
 NY, NX, NZ, NS = 4, 64, 32, 128
-K = 16
+K = 8
 XC = NX // K
-DIRECT = 2
+AHEAD = 4
+PRE = 2
+DIRECT = 1
 ZP = 8
 
 
@@ -45,11 +47,6 @@
             (vn, ve, vu)[f].at[:, cols(k)], V.at[f, :, cols(k)], v_sem.at[f, k]
         )
 
-    def store(k):
-        return pltpu.make_async_copy(
-            U.at[STEPS, :, inner(k), pl.ds(ZP, NZ)], out.at[:, cols(k)], out_sem.at[k]
-        )
-
     def y_source(first, t, side, k):
         plane = (0, NY - 1)[side]
         if first:
@@ -132,12 +129,6 @@
             device_id={"pz": 1 - pz},
             device_id_type=MESH,
         )
-
-    for i in range(K):
-        load_u(chunk(i)).start()
-    for i in range(K):
-        for f in range(3):
-            load_v(f, chunk(i)).start()
 
     barrier = pltpu.get_barrier_semaphore()
 
@@ -174,6 +165,12 @@
 
     lax.fori_loop(0, K, first_sends, 0)
 
+    for i in range(min(PRE + 2, K)):
+        load_u(chunk(i)).start()
+    for i in range(min(PRE, K)):
+        for f in range(3):
+            load_v(f, chunk(i)).start()
+
     zero_slab = pl.multiple_of(pz * (NZ + ZP), ZP)
 
     def clear_z(n, _):
@@ -192,16 +189,20 @@
     clear_x(jnp.logical_not(x_lo), 0)
     clear_x(jnp.logical_not(x_hi), NX + 1)
 
-    def compute(t, k):
+    def compute(t, k, planes):
         def column(n, _):
             x = k * XC + n
             mid = pl.ds(ZP, NZ)
-            lo = jnp.where(has_lo, H[t, 0, x], 0.0)
-            hi = jnp.where(has_hi, H[t, 1, x], 0.0)
-            c = [U[t, y, x + 1, mid, :] for y in range(NY)]
-            around = [lo] + c + [hi]
-            for y in range(NY):
-                below, above = around[y], around[y + 2]
+            for y in planes:
+                here = U[t, y, x + 1, mid, :]
+                if y == 0:
+                    below = jnp.where(has_lo, H[t, 0, x], 0.0)
+                else:
+                    below = U[t, y - 1, x + 1, mid, :]
+                if y == NY - 1:
+                    above = jnp.where(has_hi, H[t, 1, x], 0.0)
+                else:
+                    above = U[t, y + 1, x + 1, mid, :]
                 left, right = U[t, y, x, mid, :], U[t, y, x + 2, mid, :]
                 down = U[t, y, x + 1, pl.ds(ZP - 1, NZ), :]
                 up = U[t, y, x + 1, pl.ds(ZP + 1, NZ), :]
@@ -211,8 +212,17 @@
                     + V[1, y, x] * (right - left)
                     + V[2, y, x] * (up - down)
                 )
-                spread = total - 6.0 * c[y]
-                U[t + 1, y, x + 1, mid, :] = (c[y] - flow) + 0.05 * spread
+                spread = total - 6.0 * here
+                new = (here - flow) + 0.05 * spread
+
+                @pl.when(t + 1 < STEPS)
+                def _():
+                    U[jnp.minimum(t + 1, STEPS - 1), y, x + 1, mid, :] = new
+
+                @pl.when(t + 1 == STEPS)
+                def _():
+                    out[y, x] = new
+
             return 0
 
         lax.fori_loop(0, XC, column, 0)
@@ -234,22 +244,36 @@
             def _():
                 x_copy(False, t + 1, 1).start()
 
-        @pl.when(t + 1 == STEPS)
-        def _():
-            store(k).start()
+
+    def relay(n, due):
+        t, i = n // K, n % K
+
+        @pl.when(due & edge & through(t, i))
+        def _():
+            k = chunk(i)
+            slot = jnp.where(py == 0, 0, 1)
+            y_landed(t, slot, k).wait_recv()
+            relay_copy(t, k).start()
 
     def iteration(j, _):
         t, i = j // K, j % K
         k = chunk(i)
 
-        @pl.when(edge & through(t, i))
-        def _():
-            slot = jnp.where(py == 0, 0, 1)
-            y_landed(t, slot, k).wait_recv()
-            relay_copy(t, k).start()
+        relay(2 * j, j < K - AHEAD)
+        relay(2 * j + 1, j < K - AHEAD)
+        relay(j + K - AHEAD, (j >= K - AHEAD) & (j + K - AHEAD < STEPS * K))
 
         @pl.when(t == 0)
         def _():
+            @pl.when(i + PRE + 2 < K)
+            def _():
+                load_u(chunk(jnp.minimum(i + PRE + 2, K - 1))).start()
+
+            @pl.when(i + PRE < K)
+            def _():
+                for f in range(3):
+                    load_v(f, chunk(jnp.minimum(i + PRE, K - 1))).start()
+
             @pl.when(i == 0)
             def _():
                 load_u(chunk(0)).wait()
@@ -280,12 +304,9 @@
         def _():
             y_landed(t, 1, k).wait_recv()
 
-        compute(t, k)
-
-        @pl.when(j > 0)
-        def _():
-            sends(jnp.maximum(j - 1, 0))
-
+        compute(t, k, (0, NY - 1))
+        compute(t, k, range(1, NY - 1))
+        sends(j)
         return 0
 
     def x_landed(t, side):
@@ -300,7 +321,6 @@
         )
 
     lax.fori_loop(0, STEPS * K, iteration, 0)
-    sends(STEPS * K - 1)
 
     def finish(j, _):
         t, i = j // K, j % K
@@ -325,22 +345,16 @@
             def _():
                 x_landed(t, side).wait_send()
 
-    def stored(k, _):
-        store(k).wait()
-        return 0
-
-    lax.fori_loop(0, K, stored, 0)
-
 
 def body(u, vn, ve, vu):
     DMA = pltpu.SemaphoreType.DMA
-    return pl.pallas_call(
+    held = pl.pallas_call(
         kernel,
-        out_shape=jax.ShapeDtypeStruct(u.shape, u.dtype),
+        out_shape=pltpu.VMEM(u.shape, u.dtype),
         in_specs=[pl.BlockSpec(memory_space=pl.ANY)] * 4,
-        out_specs=pl.BlockSpec(memory_space=pl.ANY),
+        out_specs=pl.BlockSpec(memory_space=pltpu.VMEM),
         scratch_shapes=[
-            pltpu.VMEM((STEPS + 1, NY, NX + 2, NZ + 2 * ZP, NS), jnp.float32),
+            pltpu.VMEM((STEPS, NY, NX + 2, NZ + 2 * ZP, NS), jnp.float32),
             pltpu.VMEM((3, NY, NX, NZ, NS), jnp.float32),
             pltpu.VMEM((STEPS, 2, NX, NZ, NS), jnp.float32),
             DMA((K,)),
@@ -354,10 +368,11 @@
             DMA((STEPS, K)),
         ],
         compiler_params=pltpu.CompilerParams(
-            collective_id=0, has_side_effects=True, vmem_limit_bytes=62 * 2**20
+            collective_id=0, has_side_effects=True, vmem_limit_bytes=52 * 2**20
         ),
         name="march",
     )(u, vn, ve, vu)
+    return held
 
 
 def solution(mesh):

time: 114 us -> 109 us (0.956)
  Pallas kernels: 109 us -> 106 us
  local copies, waits for them, and re-layouts: 4.64 us -> 2.02 us
    unnamed x1, local copies, waits for them, and re-layouts: 4.64 us -> 2.02 us
    pallas_call x1, Pallas kernels: 109 us -> 106 us  [body(): pl.pallas_call(kernel, out_shape=pltpu.VMEM(u.shape, u.dtype), in_specs=[...]
where the time goes in v2:
time: 109 us
  Pallas kernels  106 us (97%)
  local copies, waits for them, and re-layouts  2.02 us (2%)
    pallas_call x1, Pallas kernels, body(): pl.pallas_call(kernel, out_shape=pltpu.VMEM(u.shape, u.dtype), in_specs=[...  106 us

profile of v2, /device:TPU:160, one launch (start us, length us, event | category | flops | bytes accessed | tf_op | source)
XLA Modules:
  0.0 108.5 jit_solution(2944074793870685827)
XLA Ops:
  0.0 106.5 %march.1 = f32[4,64,32,128]{3,2,1,0:T(8,128)S(1)} custom-call(f32[4,64,32,128]{3,2,1,0:T(8,128)} %u.1, f32[4,64,32,128]{3,2,1,0:T(8,128)} %vn.1, f32[4,64,32,128]{3,2,1,0:T(8,128)} %ve.1, f32[4,64,32,128]{3,2,1,0:T(8,128)} %vu.1), custom_call_target="tpu_custom_call" | custom-call | tf_op jit(solution)/shard_map/march/pallas_call | solution.py:351
  106.5 2.0 %copy.6 = f32[4,64,32,128]{3,2,1,0:T(8,128)} copy(f32[4,64,32,128]{3,2,1,0:T(8,128)S(1)} %march.1) | data formatting | bytes 8388608

commit v3 on v2

--- a/solution.py
+++ b/solution.py
@@ -12,14 +12,18 @@
 NY, NX, NZ, NS = 4, 64, 32, 128
 K = 8
 XC = NX // K
-AHEAD = 4
+AHEAD = 2
 PRE = 2
-DIRECT = 1
+DIRECT = 0
+DET0 = 1
+DET1 = 1
+DJ = 2
+DMAX = max(DET0, DET1, 1)
 ZP = 8
 
 
-def kernel(u, vn, ve, vu, out, U, V, H, *sems):
-    (u_sem, v_sem, out_sem, h_send, h_recv, x_send, x_recv, z_send, z_recv) = sems
+def kernel(u, vn, ve, vu, out, U, V, H, D, *sems):
+    (u_sem, v_sem, h_send, h_recv, x_send, x_recv, z_send, z_recv, d_send, d_recv) = sems
     py, px, pz = lax.axis_index("py"), lax.axis_index("px"), lax.axis_index("pz")
     has_lo, has_hi = py > 0, py < 7
     x_lo, x_hi = px > 0, px < 3
@@ -65,19 +69,62 @@
 
     def through(t, i):
         late = (t == STEPS - 1) & (i >= K - DIRECT)
-        return relayed & jnp.logical_not(late)
+        return relayed & jnp.logical_not(late) & jnp.logical_not(detoured(t, i))
+
+    def detoured(t, i):
+        return (t == 0) & (i >= K - jnp.where(pz == 0, DET0, DET1))
+
 
     def y_route(t, i, side):
         if side == 0:
             return jnp.where((py == 4) & through(t, i), 7, jnp.maximum(py - 1, 0)), 1
         return jnp.where((py == 3) & through(t, i), 0, jnp.minimum(py + 1, 7)), 0
 
+    def detour_copy(n):
+        k = chunk(K - 1 - n)
+        up = py == 3
+        return pltpu.make_async_remote_copy(
+            src_ref=u.at[jnp.where(up, NY - 1, 0), cols(k)],
+            dst_ref=D.at[n],
+            send_sem=h_send.at[0, jnp.where(up, 1, 0), k],
+            recv_sem=d_recv.at[n],
+            device_id={"py": jnp.where(up, 2, 5)},
+            device_id_type=MESH,
+        )
+
+    def pass_copy(n):
+        k = chunk(K - 1 - n)
+        slot = jnp.where(py == 2, 0, 1)
+        return pltpu.make_async_remote_copy(
+            src_ref=D.at[n],
+            dst_ref=H.at[0, slot, cols(k)],
+            send_sem=d_send.at[n],
+            recv_sem=h_recv.at[0, slot, k],
+            device_id={"py": jnp.where(py == 2, 4, 3)},
+            device_id_type=MESH,
+        )
+
+    def detour_landed(n):
+        return pltpu.make_async_remote_copy(
+            src_ref=D.at[n],
+            dst_ref=D.at[n],
+            send_sem=d_send.at[n],
+            recv_sem=d_recv.at[n],
+            device_id={"py": jnp.where(py == 2, 4, 3)},
+            device_id_type=MESH,
+        )
+
+    beside = (py == 2) | (py == 5)
+    detours = jnp.where(pz == 0, DET0, DET1)
+
     def send_y(first, t, i, k):
-        @pl.when(has_lo)
+        skip = detoured(t, i) & first
+
+        @pl.when(has_lo & ~(skip & (py == 4)))
         def _():
             y_copy(first, t, 0, k, *y_route(t, i, 0)).start()
 
-        @pl.when(has_hi)
+        @pl.when(has_hi & ~(skip & (py == 3)))
         def _():
             y_copy(first, t, 1, k, *y_route(t, i, 1)).start()
 
@@ -137,16 +184,21 @@
         def _():
             pl.semaphore_signal(barrier, inc=1, device_id=where, device_id_type=MESH)
 
-    greet(has_lo, py=jnp.maximum(py - 1, 0))
-    greet(has_hi, py=jnp.minimum(py + 1, 7))
+    meets = jnp.logical_not(relayed) | (DIRECT > 0)
+    low = has_lo & ((py != 4) | meets)
+    high = has_hi & ((py != 3) | meets)
+    greet(low, py=jnp.maximum(py - 1, 0))
+    greet(high, py=jnp.minimum(py + 1, 7))
     greet(x_lo, px=jnp.maximum(px - 1, 0))
     greet(x_hi, px=jnp.minimum(px + 1, 3))
     greet(pz >= 0, pz=1 - pz)
-    extra = relayed & (edge | middle)
-    greet(extra, py=jnp.where(edge, 3, 0))
-    greet(extra, py=jnp.where(edge, 4, 7))
+    ring = relayed & (edge | middle)
+    source = jnp.where(py == 0, 3, jnp.where(py == 4, 0, jnp.where(py == 7, 4, 7)))
+    greet(ring, py=source)
+    greet(middle & (detours > 0), py=jnp.where(py == 4, 2, 5))
     one = lambda c: c.astype(jnp.int32)
-    peers = one(has_lo) + one(has_hi) + one(x_lo) + one(x_hi) + 1 + 2 * one(extra)
+    peers = one(low) + one(high) + one(x_lo) + one(x_hi) + 1 + one(ring)
+    peers = peers + one(beside & (detours > 0))
     pl.semaphore_wait(barrier, peers)
 
     @pl.when(x_lo)
@@ -156,6 +208,12 @@
     @pl.when(x_hi)
     def _():
         x_copy(True, 0, 1).start()
+
+    for n in range(DMAX):
+
+        @pl.when(middle & (n < detours))
+        def _():
+            detour_copy(n).start()
 
     def first_sends(i, _):
         k = chunk(i)
@@ -189,7 +247,7 @@
     clear_x(jnp.logical_not(x_lo), 0)
     clear_x(jnp.logical_not(x_hi), NX + 1)
 
-    def compute(t, k, planes):
+    def compute(t, k, planes, last):
         def column(n, _):
             x = k * XC + n
             mid = pl.ds(ZP, NZ)
@@ -214,36 +272,27 @@
                 )
                 spread = total - 6.0 * here
                 new = (here - flow) + 0.05 * spread
-
-                @pl.when(t + 1 < STEPS)
-                def _():
-                    U[jnp.minimum(t + 1, STEPS - 1), y, x + 1, mid, :] = new
-
-                @pl.when(t + 1 == STEPS)
-                def _():
+                if last:
                     out[y, x] = new
-
+                else:
+                    U[t + 1, y, x + 1, mid, :] = new
             return 0
 
-        lax.fori_loop(0, XC, column, 0)
+        lax.fori_loop(0, XC, column, 0, unroll=2)
 
     def sends(j):
         t, i = j // K, j % K
         k = chunk(i)
-
-        @pl.when(t + 1 < STEPS)
-        def _():
-            send_y(False, t + 1, i, k)
-            z_copy(False, t + 1, k).start()
-
-            @pl.when((i == 0) & x_lo)
-            def _():
-                x_copy(False, t + 1, 0).start()
-
-            @pl.when((i == 1) & x_hi)
-            def _():
-                x_copy(False, t + 1, 1).start()
-
+        send_y(False, t + 1, i, k)
+        z_copy(False, t + 1, k).start()
+
+        @pl.when((i == 0) & x_lo)
+        def _():
+            x_copy(False, t + 1, 0).start()
+
+        @pl.when((i == 1) & x_hi)
+        def _():
+            x_copy(False, t + 1, 1).start()
 
     def relay(n, due):
         t, i = n // K, n % K
@@ -259,6 +308,13 @@
         t, i = j // K, j % K
         k = chunk(i)
 
+        for n in range(DMAX):
+
+            @pl.when(beside & (n < detours) & (j == DJ + DMAX - 1 - n))
+            def _():
+                detour_landed(n).wait_recv()
+                pass_copy(n).start()
+
         relay(2 * j, j < K - AHEAD)
         relay(2 * j + 1, j < K - AHEAD)
         relay(j + K - AHEAD, (j >= K - AHEAD) & (j + K - AHEAD < STEPS * K))
@@ -296,6 +352,10 @@
 
         z_copy(False, t, k).wait_recv()
 
+        @pl.when(t == STEPS - 1)
+        def _():
+            compute(t, k, range(1, NY - 1), True)
+
         @pl.when(has_lo)
         def _():
             y_landed(t, 0, k).wait_recv()
@@ -304,9 +364,16 @@
         def _():
             y_landed(t, 1, k).wait_recv()
 
-        compute(t, k, (0, NY - 1))
-        compute(t, k, range(1, NY - 1))
-        sends(j)
+        @pl.when(t < STEPS - 1)
+        def _():
+            compute(t, k, (0, NY - 1), False)
+            compute(t, k, range(1, NY - 1), False)
+            sends(j)
+
+        @pl.when(t == STEPS - 1)
+        def _():
+            compute(t, k, (0, NY - 1), True)
+
         return 0
 
     def x_landed(t, side):
@@ -338,6 +405,12 @@
         return 0
 
     lax.fori_loop(0, STEPS * K, finish, 0)
+    for n in range(DMAX):
+
+        @pl.when(beside & (n < detours))
+        def _():
+            pass_copy(n).wait_send()
+
     for t in range(STEPS):
         for side, there in ((0, x_lo), (1, x_hi)):
 
@@ -357,15 +430,17 @@
             pltpu.VMEM((STEPS, NY, NX + 2, NZ + 2 * ZP, NS), jnp.float32),
             pltpu.VMEM((3, NY, NX, NZ, NS), jnp.float32),
             pltpu.VMEM((STEPS, 2, NX, NZ, NS), jnp.float32),
+            pltpu.VMEM((DMAX, XC, NZ, NS), jnp.float32),
             DMA((K,)),
             DMA((3, K)),
-            DMA((K,)),
             DMA((STEPS, 2, K)),
             DMA((STEPS, 2, K)),
             DMA((STEPS, 2)),
             DMA((STEPS, 2)),
             DMA((STEPS, K)),
             DMA((STEPS, K)),
+            DMA((DMAX,)),
+            DMA((DMAX,)),
         ],
         compiler_params=pltpu.CompilerParams(
             collective_id=0, has_side_effects=True, vmem_limit_bytes=52 * 2**20

time: 109 us -> 107 us (0.982)
  the two profiles are of different devices: /device:TPU:160 before, /device:TPU:15 now
where the time goes in v3:
time: 107 us
  Pallas kernels  105 us (98%)
  local copies, waits for them, and re-layouts  2.02 us (2%)
    pallas_call x1, Pallas kernels, body(): pl.pallas_call(kernel, out_shape=pltpu.VMEM(u.shape, u.dtype), in_specs=[...  105 us

profile of v3, /device:TPU:15, one launch (start us, length us, event | category | flops | bytes accessed | tf_op | source)
XLA Modules:
  0.0 106.9 jit_solution(6697686152934195471)
XLA Ops:
  0.0 104.9 %march.1 = f32[4,64,32,128]{3,2,1,0:T(8,128)S(1)} custom-call(f32[4,64,32,128]{3,2,1,0:T(8,128)} %u.1, f32[4,64,32,128]{3,2,1,0:T(8,128)} %vn.1, f32[4,64,32,128]{3,2,1,0:T(8,128)} %ve.1, f32[4,64,32,128]{3,2,1,0:T(8,128)} %vu.1), custom_call_target="tpu_custom_call" | custom-call | tf_op jit(solution)/shard_map/march/pallas_call | solution.py:424
  104.9 2.0 %copy.6 = f32[4,64,32,128]{3,2,1,0:T(8,128)} copy(f32[4,64,32,128]{3,2,1,0:T(8,128)S(1)} %march.1) | data formatting | bytes 8388608

commit v4 on v3

--- a/solution.py
+++ b/solution.py
@@ -14,7 +14,8 @@
 XC = NX // K
 AHEAD = 2
 PRE = 2
-DIRECT = 0
+DA = 0
+DB = 2
 DET0 = 1
 DET1 = 1
 DJ = 2
@@ -28,6 +29,11 @@
     has_lo, has_hi = py > 0, py < 7
     x_lo, x_hi = px > 0, px < 3
     relayed = pz == 1
+    site = lax.axis_index("site")
+    outer = (site == 0) | (site == 3)
+    by_a, by_b = (
+        (site >= 0) & (w > 0) & ((w != 2) | outer) & ((w != 3) | ~outer) for w in (DA, DB)
+    )
     edge = (py == 0) | (py == 7)
     middle = (py == 3) | (py == 4)
 
@@ -68,7 +74,7 @@
         )
 
     def through(t, i):
-        late = (t == STEPS - 1) & (i >= K - DIRECT)
+        late = (t == STEPS - 1) & (i == K - 1) & jnp.where((py == 3) | (py == 0), by_a, by_b)
         return relayed & jnp.logical_not(late) & jnp.logical_not(detoured(t, i))
 
     def detoured(t, i):
@@ -184,11 +190,11 @@
         def _():
             pl.semaphore_signal(barrier, inc=1, device_id=where, device_id_type=MESH)
 
-    meets = jnp.logical_not(relayed) | (DIRECT > 0)
-    low = has_lo & ((py != 4) | meets)
-    high = has_hi & ((py != 3) | meets)
-    greet(low, py=jnp.maximum(py - 1, 0))
-    greet(high, py=jnp.minimum(py + 1, 7))
+    plain = jnp.logical_not(relayed)
+    greet(has_lo & ((py != 4) | plain | by_a), py=jnp.maximum(py - 1, 0))
+    greet(has_hi & ((py != 3) | plain | by_b), py=jnp.minimum(py + 1, 7))
+    low = has_lo & ((py != 4) | plain | by_b)
+    high = has_hi & ((py != 3) | plain | by_a)
     greet(x_lo, px=jnp.maximum(px - 1, 0))
     greet(x_hi, px=jnp.minimum(px + 1, 3))
     greet(pz >= 0, pz=1 - pz)

time: 107 us -> 106 us (level)
  no operation moved by 1% of the time
where the time goes in v4:
time: 106 us
  Pallas kernels  104 us (98%)
  local copies, waits for them, and re-layouts  2.02 us (2%)
    pallas_call x1, Pallas kernels, body(): pl.pallas_call(kernel, out_shape=pltpu.VMEM(u.shape, u.dtype), in_specs=[...  104 us

profile of v4, /device:TPU:15, one launch (start us, length us, event | category | flops | bytes accessed | tf_op | source)
XLA Modules:
  0.0 106.0 jit_solution(9991300648776293879)
XLA Ops:
  0.0 104.0 %march.1 = f32[4,64,32,128]{3,2,1,0:T(8,128)S(1)} custom-call(f32[4,64,32,128]{3,2,1,0:T(8,128)} %u.1, f32[4,64,32,128]{3,2,1,0:T(8,128)} %vn.1, f32[4,64,32,128]{3,2,1,0:T(8,128)} %ve.1, f32[4,64,32,128]{3,2,1,0:T(8,128)} %vu.1), custom_call_target="tpu_custom_call" | custom-call | tf_op jit(solution)/shard_map/march/pallas_call | solution.py:430
  104.0 2.0 %copy.6 = f32[4,64,32,128]{3,2,1,0:T(8,128)} copy(f32[4,64,32,128]{3,2,1,0:T(8,128)S(1)} %march.1) | data formatting | bytes 8388608
